TPU v7x, 128 devices: a whole 4x4x4 slice. The times are simulated.
128 devices in a mesh: img: 16 (over z, y_hi, core), feat: 8 (over y_lo, x).
Axes of the slice: x: 4, y: 4 (y_hi: 2, y_lo: 2; y = y_hi * 2 + y_lo), z: 4, core: 2. Of those that a mesh axis runs over, the one named last changes fastest.
Arguments:
- features: bfloat16 [16384, 32768], P('img', 'feat'), may hold values from -0.055242717 to 0.055242717
- weights: bfloat16 [512, 32768], P('img', 'feat'), may hold values from -20 to 20
- direction: bfloat16 [512, 32768], P('img', 'feat'), may hold values from -6 to 6
Outputs:
- hessian_product: float32 [512, 32768], P('img', 'feat')
All inputs are finite; a program needn't handle non-finite values.
Results may differ from a plain program's by a relative error of at most 0.0024.
Values may be sent and summed in bfloat16 or wider, within the bound.
A program may use at most 64 MiB of HBM per device.

v0:
```python
import jax
import jax.numpy as jnp
from jax import lax
from jax.sharding import PartitionSpec as P


def in_order(parts, dim):
    shape = list(parts.shape[1:])
    shape[dim] *= parts.shape[0]
    return jnp.moveaxis(parts, 0, dim).reshape(shape)


def from_everyone(shard, axis):
    length = lax.axis_size(axis)
    return lax.all_to_all(
        jnp.broadcast_to(shard[None], (length, *shard.shape)), axis, 0, 0, tiled=True
    )


def gathered_copies(shard, axis, dim):
    return in_order(from_everyone(shard, axis), dim)


def weigh(pair):
    prob = jax.nn.sigmoid(pair[0])
    return (prob * (1.0 - prob) * pair[1]).astype(jnp.bfloat16)


def body(features, weights, direction):
    stacked = jnp.stack((weights, direction))
    partial_scores = jnp.einsum(
        "rf,kcf->krc",
        features,
        lax.all_gather(stacked, "img", axis=1, tiled=True),
        preferred_element_type=jnp.float32,
    )
    shares = lax.psum_scatter(partial_scores, "feat", scatter_dimension=1, tiled=True)
    curvature = gathered_copies(weigh(shares), "feat", 0)
    summed_terms = lax.psum_scatter(
        lax.dot_general(
            curvature, features, (((0,), (0,)), ((), ())), preferred_element_type=jnp.float32
        ),
        "img",
        scatter_dimension=0,
        tiled=True,
    )
    return 4.0 * summed_terms


def solution(mesh):
    placed = (P("img", "feat"), P("img", "feat"), P("img", "feat"))
    return jax.shard_map(
        body, mesh=mesh, in_specs=placed, out_specs=P("img", "feat"), check_vma=False
    )
```

profile of v0, /device:TPU:0, one launch (start us, length us, event | category | flops | bytes accessed | tf_op | source)
XLA Modules:
  0.0 291.0 jit_solution(6749987864184155752)
XLA Ops:
  6.5 0.0 all-gather.2.cloned.1.call-start
  6.5 1.9 pad_maximum_fusion
  8.4 0.0 all-gather.2.cloned.1.call-update
  8.4 0.0 reduce-scatter.3.cloned.1.call-start
  8.5 76.7 %all-gather.2.cloned.1.call-done = bf16[2,512,4096]{2,1,0:T(8,128)(2,1)} async-done(((bf16[2,32,4096]{2,1,0:T(8,128)(2,1)}), bf16[2,512,4096]{2,1,0:T(8,128)(2,1)}) %all-gather.2.cloned.1.call-update) | async-done | bytes 8388624 | tf_op jit(solution)/shard_map/all_gather | solution.py:34
  85.2 15.1 %fusion.2 = f32[2,1024,512]{1,2,0:T(8,128)} fusion(bf16[2,512,4096]{2,1,0:T(8,128)(2,1)} %all-gather.2.cloned.1.call-done, bf16[1024,4096]{1,0:T(8,128)(2,1)} %param.3), kind=kOutput, calls=%fused_computation.2 | convolution fusion | flops 8589934592 | bytes 20971520 | tf_op jit(solution)/shard_map/rf,kcf->krc/dot_general | solution.py:31
  100.2 0.0 reduce-scatter.3.cloned.1.call-update
  100.2 0.0 reduce-scatter.5.cloned.1.call-start
  100.3 50.8 %reduce-scatter.3.cloned.1.call-done = f32[2,128,512]{1,2,0:T(8,128)} async-done(((f32[2,1024,512]{1,2,0:T(8,128)}), f32[2,128,512]{1,2,0:T(8,128)}) %reduce-scatter.3.cloned.1.call-update) | async-done | bytes 524304 | tf_op jit(solution)/shard_map/reduce_scatter | solution.py:37
  151.1 1.1 fusion.10
  152.2 0.1 copy.4
  152.4 0.1 broadcast_in_dim.9
  152.5 18.3 %all_to_all.5 = bf16[8,128,512]{2,1,0:T(8,128)(2,1)S(1)} all-to-all(bf16[8,128,512]{2,1,0:T(8,128)(2,1)S(1)} %broadcast_in_dim.9), channel_id=1, replica_groups=mesh['img'=16,'feat'=8] {'feat'}, dimensions={0} | all-to-all | bytes 2097152 | tf_op jit(solution)/shard_map/all_to_all | solution.py:15
  170.8 10.1 %fusion.11 = f32[512,4096]{1,0:T(8,128)} fusion(bf16[1024,512]{1,0:T(8,128)(2,1)S(1)} %bitcast.15, bf16[1024,4096]{1,0:T(8,128)(2,1)} %param.3), kind=kOutput, calls=%fused_computation.13 | convolution fusion | flops 4294967296 | bytes 17825792 | tf_op jit(solution)/shard_map/dot_general | solution.py:40
  180.9 0.0 reduce-scatter.5.cloned.1.call-update
  181.0 101.6 %reduce-scatter.5.cloned.1.call-done = f32[32,4096]{1,0:T(8,128)} async-done(((f32[512,4096]{1,0:T(8,128)}), f32[32,4096]{1,0:T(8,128)}) %reduce-scatter.5.cloned.1.call-update) | async-done | bytes 524304 | tf_op jit(solution)/shard_map/reduce_scatter | solution.py:39
  282.6 1.9 broadcast_multiply_fusion
Async XLA Ops:
  6.5 78.6 %all-gather.2.cloned.1.call-start = ((), (), s32[]{:S(2)}) async-start(), calls=%async_computation.3 | async-start | bytes 8912896 | tf_op jit(solution)/shard_map/all_gather | solution.py:34
  8.4 142.7 %reduce-scatter.3.cloned.1.call-start = ((), (), s32[]{:S(2)}) async-start(), calls=%async_computation.4 | async-start | bytes 4718592 | tf_op jit(solution)/shard_map/reduce_scatter | solution.py:37
  100.2 182.4 %reduce-scatter.5.cloned.1.call-start = ((), (), s32[]{:S(2)}) async-start(), calls=%async_computation.5 | async-start | bytes 8912896 | tf_op jit(solution)/shard_map/reduce_scatter | solution.py:39
Sparse Core Ops, SparseCore 0:
  9.8 75.3 all-gather.1
  100.4 50.7 reduce-scatter.2
  181.1 101.4 reduce-scatter.4
where the time goes:
time: 291 us
  waiting for transfers between devices  229 us (79%)
  matrix products  25.2 us (9%)
  blocking collectives  18.3 us (6%)
  between operations  13.1 us (5%)
  other arithmetic  4.86 us (2%)
    reduce_scatter x1, waiting for transfers between devices, body(): lax.psum_scatter(lax.dot_general(curvature, features, (((0,), (0,)), ((),...  102 us
    all_gather x1, waiting for transfers between devices, body(): lax.all_gather(stacked, 'img', axis=1, tiled=True)  76.7 us
    reduce_scatter x1, waiting for transfers between devices, body(): lax.psum_scatter(partial_scores, 'feat', scatter_dimension=1, tiled=True)  50.8 us
    all_to_all x1, blocking collectives, from_everyone(): lax.all_to_all(jnp.broadcast_to(shard[None], (length, *shard.shape)), axi...  18.3 us
    dot_general x1, matrix products, body(): jnp.einsum('rf,kcf->krc', features, lax.all_gather(stacked, 'img', axis=1...  15.1 us
    dot_general x1, matrix products, body(): lax.dot_general(curvature, features, (((0,), (0,)), ((), ())), preferred_...  10.1 us
  transfers between devices with their start and end apart: 3, of which 3 were waited for; matrix products, arithmetic and copies ran while one was open for 0% of the time, Pallas kernels for 0%

commit v1 on v0

--- a/solution.py
+++ b/solution.py
@@ -28,11 +28,15 @@
 
 def body(features, weights, direction):
     stacked = jnp.stack((weights, direction))
+
+    def ways_start(field_in, dim_i=1):
+        return jnp.concatenate(
+            jax.lax.all_to_all(jnp.stack(jax.lax.axis_size("img") * [field_in], 0), "img", 0, 0),
+            dim_i,
+        )
+
     partial_scores = jnp.einsum(
-        "rf,kcf->krc",
-        features,
-        lax.all_gather(stacked, "img", axis=1, tiled=True),
-        preferred_element_type=jnp.float32,
+        "rf,kcf->krc", features, ways_start(stacked), preferred_element_type=jnp.float32
     )
     shares = lax.psum_scatter(partial_scores, "feat", scatter_dimension=1, tiled=True)
     curvature = gathered_copies(weigh(shares), "feat", 0)

time: 291 us -> 327 us (1.12)
  blocking collectives: 18.3 us -> 123 us
  waiting for transfers between devices: 229 us -> 152 us
  local copies, waits for them, and re-layouts: 0.2 us -> 8.97 us
    all_to_all x0 -> x1, blocking collectives: none -> 105 us  [ways_start(): jax.lax.all_to_all(jnp.stack(jax.lax.axis_size('img') * [field_in], 0), '...]
    all_gather x1 -> x0, waiting for transfers between devices: 76.7 us -> none  [body(): lax.all_gather(stacked, 'img', axis=1, tiled=True)]
    reshape x0 -> x1, local copies, waits for them, and re-layouts: none -> 7.71 us  [ways_start(): jnp.concatenate(jax.lax.all_to_all(jnp.stack(jax.lax.axis_size('img') * [...]
  transfers between devices with their start and end apart: 3 -> 2, of which waited for: 3 -> 2; matrix products, arithmetic and copies ran while one was open for 0% -> 0% of each run, Pallas kernels for 0% -> 0%
where the time goes in v1:
time: 327 us; the launch traced here: 326 us
  waiting for transfers between devices  152 us (46%)
  blocking collectives  123 us (38%)
  matrix products  25.2 us (8%)
  between operations  13.4 us (4%)
  local copies, waits for them, and re-layouts  8.97 us (3%)
  other arithmetic  4.07 us (1%)
    all_to_all x1, blocking collectives, ways_start(): jax.lax.all_to_all(jnp.stack(jax.lax.axis_size('img') * [field_in], 0), '...  105 us
    reduce_scatter x1, waiting for transfers between devices, body(): lax.psum_scatter(lax.dot_general(curvature, features, (((0,), (0,)), ((),...  102 us
    reduce_scatter x1, waiting for transfers between devices, body(): lax.psum_scatter(partial_scores, 'feat', scatter_dimension=1, tiled=True)  50 us
    all_to_all x1, blocking collectives, from_everyone(): lax.all_to_all(jnp.broadcast_to(shard[None], (length, *shard.shape)), axi...  18.4 us
    dot_general x1, matrix products, body(): jnp.einsum('rf,kcf->krc', features, ways_start(stacked), preferred_elemen...  15.1 us
    dot_general x1, matrix products, body(): lax.dot_general(curvature, features, (((0,), (0,)), ((), ())), preferred_...  10.1 us
    reshape x1, local copies, waits for them, and re-layouts, ways_start(): jnp.concatenate(jax.lax.all_to_all(jnp.stack(jax.lax.axis_size('img') * [...  7.71 us
  transfers between devices with their start and end apart: 2, of which 2 were waited for; matrix products, arithmetic and copies ran while one was open for 0% of the time, Pallas kernels for 0%

profile of v1, /device:TPU:0, one launch (start us, length us, event | category | flops | bytes accessed | tf_op | source)
XLA Modules:
  0.0 326.5 jit_solution(10309177773046937133)
XLA Ops:
  6.5 0.0 reduce-scatter.3.cloned.1.call-start
  6.5 1.1 pad_maximum_fusion
  7.6 1.1 stack.11
  8.7 104.7 %all_to_all.10 = bf16[16,2,32,4096]{3,2,1,0:T(8,128)(2,1)} all-to-all(bf16[16,2,32,4096]{3,2,1,0:T(8,128)(2,1)S(1)} %stack.11), channel_id=1, replica_groups=mesh['img'=16,'feat'=8] {'img'}, dimensions={0} | all-to-all | bytes 16777216 | tf_op jit(solution)/shard_map/all_to_all | solution.py:34
  113.4 7.7 %copy.5 = bf16[2,16,32,4096]{3,2,1,0:T(8,128)(2,1)} copy(bf16[2,16,32,4096]{3,2,0,1:T(8,128)(2,1)} %bitcast.17) | data formatting | bytes 16777216 | tf_op jit(solution)/shard_map/reshape | solution.py:33
  121.1 15.1 %fusion.2 = f32[2,1024,512]{1,2,0:T(8,128)} fusion(bf16[2,512,4096]{2,1,0:T(8,128)(2,1)} %bitcast.18, bf16[1024,4096]{1,0:T(8,128)(2,1)} %param.3), kind=kOutput, calls=%fused_computation.2 | convolution fusion | flops 8589934592 | bytes 20971520 | tf_op jit(solution)/shard_map/rf,kcf->krc/dot_general | solution.py:38
  136.1 0.0 reduce-scatter.3.cloned.1.call-update
  136.2 0.0 reduce-scatter.5.cloned.1.call-start
  136.2 50.0 %reduce-scatter.3.cloned.1.call-done = f32[2,128,512]{1,2,0:T(8,128)} async-done(((f32[2,1024,512]{1,2,0:T(8,128)}), f32[2,128,512]{1,2,0:T(8,128)}) %reduce-scatter.3.cloned.1.call-update) | async-done | bytes 524304 | tf_op jit(solution)/shard_map/reduce_scatter | solution.py:41
  186.2 1.1 fusion.10
  187.3 0.1 copy.6
  187.4 0.1 broadcast_in_dim.9
  187.5 18.4 %all_to_all.11 = bf16[8,128,512]{2,1,0:T(8,128)(2,1)S(1)} all-to-all(bf16[8,128,512]{2,1,0:T(8,128)(2,1)S(1)} %broadcast_in_dim.9), channel_id=1, replica_groups=mesh['img'=16,'feat'=8] {'feat'}, dimensions={0} | all-to-all | bytes 2097152 | tf_op jit(solution)/shard_map/all_to_all | solution.py:15
  205.9 10.1 %fusion.11 = f32[512,4096]{1,0:T(8,128)} fusion(bf16[1024,512]{1,0:T(8,128)(2,1)S(1)} %bitcast.19, bf16[1024,4096]{1,0:T(8,128)(2,1)} %param.3), kind=kOutput, calls=%fused_computation.13 | convolution fusion | flops 4294967296 | bytes 17825792 | tf_op jit(solution)/shard_map/dot_general | solution.py:44
  216.0 0.0 reduce-scatter.5.cloned.1.call-update
  216.0 101.7 %reduce-scatter.5.cloned.1.call-done = f32[32,4096]{1,0:T(8,128)} async-done(((f32[512,4096]{1,0:T(8,128)}), f32[32,4096]{1,0:T(8,128)}) %reduce-scatter.5.cloned.1.call-update) | async-done | bytes 524304 | tf_op jit(solution)/shard_map/reduce_scatter | solution.py:43
  317.7 1.9 broadcast_multiply_fusion
Async XLA Ops:
  6.5 179.6 %reduce-scatter.3.cloned.1.call-start = ((), (), s32[]{:S(2)}) async-start(), calls=%async_computation.4 | async-start | bytes 4718592 | tf_op jit(solution)/shard_map/reduce_scatter | solution.py:41
  136.2 181.6 %reduce-scatter.5.cloned.1.call-start = ((), (), s32[]{:S(2)}) async-start(), calls=%async_computation.5 | async-start | bytes 8912896 | tf_op jit(solution)/shard_map/reduce_scatter | solution.py:43
Sparse Core Ops, SparseCore 0:
  136.3 49.8 reduce-scatter.2
  216.2 101.5 reduce-scatter.4
